TPU v7x, 32 devices: a whole 2x2x4 slice. The times are simulated.
32 devices in a mesh: freq: 2 (over x), base: 4 (over y, core), pix: 4 (over z).
Axes of the slice: x: 2, y: 2, z: 4, core: 2. Of those that a mesh axis runs over, the one named last changes fastest.
Arguments:
- sensing_operator_parts: bfloat16 [2, 4096, 2048], P('freq', 'base', 'pix'), may hold values from -1 to 1
- sampled_correlations: float32 [64, 4096], P('freq', 'base'), may hold values from -40 to 40
- first_sky_estimate: float32 [64, 4, 4, 128], P('freq', 'pix', 'base'), may hold values from -2.5 to 2.5
- patch_order_record: int32 [6, 16], P(None, 'pix'), may hold values from 0 to 15, as said below
Outputs:
- image: float32 [64, 4, 4, 128], P('freq', 'pix', 'base')
Inputs may be any that keep to these rules, and one draw needn't show every extreme that they name: `patch_order_record`: each row holds every tile number once; the tiles of rank under 4 are the same in every row.
All inputs are finite; a program needn't handle non-finite values.
Results may differ from a plain program's by a relative error of at most 0.0014.
Values may be sent and summed in bfloat16 or wider, within the bound.
No kernel may reach another device: no remote copies, remote signals or barrier semaphores. Data moves between devices by JAX's collectives and lax.ppermute only.
A program may use at most 64 MiB of HBM per device.

v0:
```python
import jax
import jax.numpy as jnp
from jax import lax
from jax.sharding import PartitionSpec as P

CH = 64
TILE = 128
ITERS = 6
descent_stride = 0.6
lam_shrink = 0.3
eps_norm = 1e-06


def project_rows(rounded_amount, columns):
    return lax.dot_general(
        rounded_amount, columns, (((1,), (1,)), ((), ())), preferred_element_type=jnp.float32
    )


def residual_of(sampled_correlations, partial_value):
    shares = lax.psum_scatter(partial_value, "pix", scatter_dimension=1, tiled=True)
    width = shares.shape[1]
    own_rows = lax.dynamic_slice_in_dim(
        sampled_correlations, lax.axis_index("pix") * width, width, 1
    )
    return lax.all_gather((own_rows - shares).astype(jnp.bfloat16), "pix", axis=1, tiled=True)


def on_device(sensing_operator_parts, sampled_correlations, first_sky_estimate, patch_order_record):
    sensing_operator = sensing_operator_parts[0]
    chans, m_dev = sampled_correlations.shape
    share_width = first_sky_estimate.shape[3]
    tiles_share = share_width // TILE
    keep_count = tiles_share * lax.axis_size("base") * lax.axis_size("pix") // 4
    base_index = lax.axis_index("base")
    own_share = first_sky_estimate[:, 0, 0, :]
    current = own_share
    for step in range(ITERS):
        rounded_amount = current.astype(jnp.bfloat16)
        partial_value = project_rows(
            lax.all_gather(rounded_amount, "base", axis=1, tiled=True), sensing_operator
        )
        resid = residual_of(sampled_correlations, partial_value)
        gradient_portion = jnp.dot(resid, sensing_operator, preferred_element_type=jnp.float32)
        grad_share = lax.psum_scatter(gradient_portion, "base", scatter_dimension=1, tiled=True)
        moved = current + descent_stride * grad_share
        tiles = moved.reshape(chans, tiles_share, TILE)
        local_sum = jnp.sum(tiles * tiles, axis=(0, 2))
        total = lax.psum(local_sum, "freq")
        ranks = lax.dynamic_slice_in_dim(
            patch_order_record[step], base_index * tiles_share, tiles_share, 0
        )
        rms_tile = jnp.sqrt(total / (CH * TILE) + eps_norm)
        keeping = (ranks < keep_count).astype(jnp.float32)
        factor = keeping * rms_tile / (rms_tile + lam_shrink)
        current = (tiles * factor[None, :, None]).reshape(chans, share_width)
    return current.reshape(chans, 1, 1, share_width)


def solution(mesh):
    in_specs = (
        P("freq", "base", "pix"),
        P("freq", "base"),
        P("freq", "pix", "base", None),
        P(None, "pix"),
    )
    out_specs = P("freq", "pix", "base", None)
    return jax.shard_map(
        on_device, mesh=mesh, in_specs=in_specs, out_specs=out_specs, check_vma=False
    )
```

profile of v0, /device:TPU:0, one launch (start us, length us, event | category | flops | bytes accessed | tf_op | source)
XLA Modules:
  0.0 418.8 jit_solution(5193370528719612826)
XLA Ops:
  7.3 6.1 %all_gather.36 = bf16[32,512]{1,0:T(8,128)(2,1)S(1)} all-gather(bf16[32,128]{1,0:T(8,128)(2,1)S(1)} %convert_element_type.42), channel_id=1, replica_groups=mesh['freq'=2,'base'=4,'pix'=4] {'base'}, dimensions={1}, use_global_device_ids=true | all-gather | bytes 40960 | tf_op jit(solution)/shard_map/all_gather | solution.py:41
  14.6 21.3 %reduce-scatter.13.cloned.1.call-done = f32[32,256]{1,0:T(8,128)} async-done(((f32[32,1024]{1,0:T(8,128)}), f32[32,256]{1,0:T(8,128)}) %reduce-scatter.13.cloned.1.call-update) | async-done | bytes 32784 | tf_op jit(solution)/shard_map/reduce_scatter | solution.py:21
  36.7 13.1 %all_gather.37 = bf16[32,1024]{1,0:T(8,128)(2,1)S(1)} all-gather(bf16[32,256]{1,0:T(8,128)(2,1)S(1)} %subtract_convert_fusion.5), channel_id=1, replica_groups=mesh['freq'=2,'base'=4,'pix'=4] {'pix'}, dimensions={1}, use_global_device_ids=true | all-gather | bytes 81920 | tf_op jit(solution)/shard_map/all_gather | solution.py:26
  52.0 16.6 %reduce-scatter.15.cloned.1.call-done = f32[32,128]{1,0:T(8,128)} async-done(((f32[32,512]{1,0:T(8,128)}), f32[32,128]{1,0:T(8,128)}) %reduce-scatter.15.cloned.1.call-update) | async-done | bytes 16400 | tf_op jit(solution)/shard_map/reduce_scatter | solution.py:45
  68.6 1.4 multiply_reduce_fusion.5
  70.0 5.5 %psum.42 = f32[1]{0:T(128)} all-reduce(f32[1]{0:T(128)} %bitcast.3), channel_id=1, replica_groups=mesh['freq'=2,'base'=4,'pix'=4] {'freq'}, use_global_device_ids=true, to_apply=%region_3.0 | all-reduce | flops 1 | bytes 8 | tf_op jit(solution)/shard_map/psum | solution.py:49
  76.9 5.2 %all_gather.38 = bf16[32,512]{1,0:T(8,128)(2,1)S(1)} all-gather(bf16[32,128]{1,0:T(8,128)(2,1)S(1)} %multiply_convert_fusion.4), channel_id=1, replica_groups=mesh['freq'=2,'base'=4,'pix'=4] {'base'}, dimensions={1}, use_global_device_ids=true | all-gather | bytes 40960 | tf_op jit(solution)/shard_map/all_gather | solution.py:41
  83.2 19.6 %reduce-scatter.17.cloned.1.call-done = f32[32,256]{1,0:T(8,128)} async-done(((f32[32,1024]{1,0:T(8,128)}), f32[32,256]{1,0:T(8,128)}) %reduce-scatter.17.cloned.1.call-update) | async-done | bytes 32784 | tf_op jit(solution)/shard_map/reduce_scatter | solution.py:21
  103.5 13.1 %all_gather.39 = bf16[32,1024]{1,0:T(8,128)(2,1)S(1)} all-gather(bf16[32,256]{1,0:T(8,128)(2,1)S(1)} %subtract_convert_fusion.4), channel_id=1, replica_groups=mesh['freq'=2,'base'=4,'pix'=4] {'pix'}, dimensions={1}, use_global_device_ids=true | all-gather | bytes 81920 | tf_op jit(solution)/shard_map/all_gather | solution.py:26
  118.2 17.3 %reduce-scatter.19.cloned.1.call-done = f32[32,128]{1,0:T(8,128)} async-done(((f32[32,512]{1,0:T(8,128)}), f32[32,128]{1,0:T(8,128)}) %reduce-scatter.19.cloned.1.call-update) | async-done | bytes 16400 | tf_op jit(solution)/shard_map/reduce_scatter | solution.py:45
  135.5 1.4 multiply_reduce_fusion.4
  136.9 5.5 %psum.43 = f32[1]{0:T(128)} all-reduce(f32[1]{0:T(128)} %bitcast.6), channel_id=1, replica_groups=mesh['freq'=2,'base'=4,'pix'=4] {'freq'}, use_global_device_ids=true, to_apply=%region_7.0 | all-reduce | flops 1 | bytes 8 | tf_op jit(solution)/shard_map/psum | solution.py:49
  143.8 5.2 %all_gather.40 = bf16[32,512]{1,0:T(8,128)(2,1)S(1)} all-gather(bf16[32,128]{1,0:T(8,128)(2,1)S(1)} %multiply_convert_fusion.3), channel_id=1, replica_groups=mesh['freq'=2,'base'=4,'pix'=4] {'base'}, dimensions={1}, use_global_device_ids=true | all-gather | bytes 40960 | tf_op jit(solution)/shard_map/all_gather | solution.py:41
  150.1 19.6 %reduce-scatter.21.cloned.1.call-done = f32[32,256]{1,0:T(8,128)} async-done(((f32[32,1024]{1,0:T(8,128)}), f32[32,256]{1,0:T(8,128)}) %reduce-scatter.21.cloned.1.call-update) | async-done | bytes 32784 | tf_op jit(solution)/shard_map/reduce_scatter | solution.py:21
  170.5 13.1 %all_gather.41 = bf16[32,1024]{1,0:T(8,128)(2,1)S(1)} all-gather(bf16[32,256]{1,0:T(8,128)(2,1)S(1)} %subtract_convert_fusion.3), channel_id=1, replica_groups=mesh['freq'=2,'base'=4,'pix'=4] {'pix'}, dimensions={1}, use_global_device_ids=true | all-gather | bytes 81920 | tf_op jit(solution)/shard_map/all_gather | solution.py:26
  185.1 17.3 %reduce-scatter.23.cloned.1.call-done = f32[32,128]{1,0:T(8,128)} async-done(((f32[32,512]{1,0:T(8,128)}), f32[32,128]{1,0:T(8,128)}) %reduce-scatter.23.cloned.1.call-update) | async-done | bytes 16400 | tf_op jit(solution)/shard_map/reduce_scatter | solution.py:45
  203.8 5.5 %psum.44 = f32[1]{0:T(128)} all-reduce(f32[1]{0:T(128)} %bitcast.9), channel_id=1, replica_groups=mesh['freq'=2,'base'=4,'pix'=4] {'freq'}, use_global_device_ids=true, to_apply=%region_11.0 | all-reduce | flops 1 | bytes 8 | tf_op jit(solution)/shard_map/psum | solution.py:49
  210.7 5.2 %all_gather.42 = bf16[32,512]{1,0:T(8,128)(2,1)S(1)} all-gather(bf16[32,128]{1,0:T(8,128)(2,1)S(1)} %multiply_convert_fusion.2), channel_id=1, replica_groups=mesh['freq'=2,'base'=4,'pix'=4] {'base'}, dimensions={1}, use_global_device_ids=true | all-gather | bytes 40960 | tf_op jit(solution)/shard_map/all_gather | solution.py:41
  217.0 19.6 %reduce-scatter.25.cloned.1.call-done = f32[32,256]{1,0:T(8,128)} async-done(((f32[32,1024]{1,0:T(8,128)}), f32[32,256]{1,0:T(8,128)}) %reduce-scatter.25.cloned.1.call-update) | async-done | bytes 32784 | tf_op jit(solution)/shard_map/reduce_scatter | solution.py:21
  237.3 13.1 %all_gather.43 = bf16[32,1024]{1,0:T(8,128)(2,1)S(1)} all-gather(bf16[32,256]{1,0:T(8,128)(2,1)S(1)} %subtract_convert_fusion.2), channel_id=1, replica_groups=mesh['freq'=2,'base'=4,'pix'=4] {'pix'}, dimensions={1}, use_global_device_ids=true | all-gather | bytes 81920 | tf_op jit(solution)/shard_map/all_gather | solution.py:26
  252.0 17.3 %reduce-scatter.27.cloned.1.call-done = f32[32,128]{1,0:T(8,128)} async-done(((f32[32,512]{1,0:T(8,128)}), f32[32,128]{1,0:T(8,128)}) %reduce-scatter.27.cloned.1.call-update) | async-done | bytes 16400 | tf_op jit(solution)/shard_map/reduce_scatter | solution.py:45
  270.7 5.5 %psum.45 = f32[1]{0:T(128)} all-reduce(f32[1]{0:T(128)} %bitcast.12), channel_id=1, replica_groups=mesh['freq'=2,'base'=4,'pix'=4] {'freq'}, use_global_device_ids=true, to_apply=%region_15.0 | all-reduce | flops 1 | bytes 8 | tf_op jit(solution)/shard_map/psum | solution.py:49
  277.6 5.2 %all_gather.44 = bf16[32,512]{1,0:T(8,128)(2,1)S(1)} all-gather(bf16[32,128]{1,0:T(8,128)(2,1)S(1)} %multiply_convert_fusion.1), channel_id=1, replica_groups=mesh['freq'=2,'base'=4,'pix'=4] {'base'}, dimensions={1}, use_global_device_ids=true | all-gather | bytes 40960 | tf_op jit(solution)/shard_map/all_gather | solution.py:41
  283.9 19.6 %reduce-scatter.29.cloned.1.call-done = f32[32,256]{1,0:T(8,128)} async-done(((f32[32,1024]{1,0:T(8,128)}), f32[32,256]{1,0:T(8,128)}) %reduce-scatter.29.cloned.1.call-update) | async-done | bytes 32784 | tf_op jit(solution)/shard_map/reduce_scatter | solution.py:21
  304.2 13.1 %all_gather.45 = bf16[32,1024]{1,0:T(8,128)(2,1)S(1)} all-gather(bf16[32,256]{1,0:T(8,128)(2,1)S(1)} %subtract_convert_fusion.1), channel_id=1, replica_groups=mesh['freq'=2,'base'=4,'pix'=4] {'pix'}, dimensions={1}, use_global_device_ids=true | all-gather | bytes 81920 | tf_op jit(solution)/shard_map/all_gather | solution.py:26
  318.9 17.3 %reduce-scatter.31.cloned.1.call-done = f32[32,128]{1,0:T(8,128)} async-done(((f32[32,512]{1,0:T(8,128)}), f32[32,128]{1,0:T(8,128)}) %reduce-scatter.31.cloned.1.call-update) | async-done | bytes 16400 | tf_op jit(solution)/shard_map/reduce_scatter | solution.py:45
  337.6 5.5 %psum.46 = f32[1]{0:T(128)} all-reduce(f32[1]{0:T(128)} %bitcast.15), channel_id=1, replica_groups=mesh['freq'=2,'base'=4,'pix'=4] {'freq'}, use_global_device_ids=true, to_apply=%region_19.0 | all-reduce | flops 1 | bytes 8 | tf_op jit(solution)/shard_map/psum | solution.py:49
  344.5 5.2 %all_gather.46 = bf16[32,512]{1,0:T(8,128)(2,1)S(1)} all-gather(bf16[32,128]{1,0:T(8,128)(2,1)S(1)} %multiply_convert_fusion), channel_id=1, replica_groups=mesh['freq'=2,'base'=4,'pix'=4] {'base'}, dimensions={1}, use_global_device_ids=true | all-gather | bytes 40960 | tf_op jit(solution)/shard_map/all_gather | solution.py:41
  350.8 19.6 %reduce-scatter.33.cloned.1.call-done = f32[32,256]{1,0:T(8,128)} async-done(((f32[32,1024]{1,0:T(8,128)}), f32[32,256]{1,0:T(8,128)}) %reduce-scatter.33.cloned.1.call-update) | async-done | bytes 32784 | tf_op jit(solution)/shard_map/reduce_scatter | solution.py:21
  371.1 13.1 %all_gather.47 = bf16[32,1024]{1,0:T(8,128)(2,1)S(1)} all-gather(bf16[32,256]{1,0:T(8,128)(2,1)S(1)} %subtract_convert_fusion), channel_id=1, replica_groups=mesh['freq'=2,'base'=4,'pix'=4] {'pix'}, dimensions={1}, use_global_device_ids=true | all-gather | bytes 81920 | tf_op jit(solution)/shard_map/all_gather | solution.py:26
  385.7 17.4 %reduce-scatter.35.cloned.1.call-done = f32[32,128]{1,0:T(8,128)} async-done(((f32[32,512]{1,0:T(8,128)}), f32[32,128]{1,0:T(8,128)}) %reduce-scatter.35.cloned.1.call-update) | async-done | bytes 16400 | tf_op jit(solution)/shard_map/reduce_scatter | solution.py:45
  404.5 5.5 %psum.47 = f32[1]{0:T(128)} all-reduce(f32[1]{0:T(128)} %bitcast.18), channel_id=1, replica_groups=mesh['freq'=2,'base'=4,'pix'=4] {'freq'}, use_global_device_ids=true, to_apply=%region_23.0 | all-reduce | flops 1 | bytes 8 | tf_op jit(solution)/shard_map/psum | solution.py:49
  (72 shorter events, 27.9 us)
Async XLA Ops:
  6.5 7.0 %copy-start = (bf16[1,1024,512]{2,1,0:T(8,128)(2,1)S(1)}, bf16[1,1024,512]{2,1,0:T(8,128)(2,1)}, u32[]{:S(2)}) copy-start(bf16[1,1024,512]{2,1,0:T(8,128)(2,1)} %param.4) | copy-start | bytes 3145732
  6.5 29.4 %reduce-scatter.13.cloned.1.call-start = ((), (), s32[]{:S(2)}) async-start(), calls=%async_computation.12 | async-start | bytes 163840 | tf_op jit(solution)/shard_map/reduce_scatter | solution.py:21
  14.5 21.4 %copy-start.1 = (f32[32,1024]{1,0:T(8,128)S(1)}, f32[32,1024]{1,0:T(8,128)}, u32[]{:S(2)}) copy-start(f32[32,1024]{1,0:T(8,128)} %param.5) | copy-start | bytes 393220
  14.6 54.1 %reduce-scatter.15.cloned.1.call-start = ((), (), s32[]{:S(2)}) async-start(), calls=%async_computation.13 | async-start | bytes 81920 | tf_op jit(solution)/shard_map/reduce_scatter | solution.py:45
  50.7 0.7 copy-start.4
  50.7 17.9 %copy-start.2 = (f32[32,1,1,128]{3,2,1,0:T(1,128)S(1)}, f32[32,1,1,128]{3,2,1,0:T(1,128)}, u32[]{:S(2)}) copy-start(f32[32,1,1,128]{3,2,1,0:T(1,128)} %param.6) | copy-start | bytes 49156
  50.8 52.0 %reduce-scatter.17.cloned.1.call-start = ((), (), s32[]{:S(2)}) async-start(), calls=%async_computation.14 | async-start | bytes 163840 | tf_op jit(solution)/shard_map/reduce_scatter | solution.py:21
  70.0 6.8 %copy-start.3 = (f32[32,128]{1,0:T(8,128)S(1)}, f32[32,128]{1,0:T(8,128)}, u32[]{:S(2)}) copy-start(f32[32,128]{1,0:T(8,128)} %reduce-scatter.15.cloned.1.call-done) | copy-start | bytes 49156
  83.2 52.3 %reduce-scatter.19.cloned.1.call-start = ((), (), s32[]{:S(2)}) async-start(), calls=%async_computation.15 | async-start | bytes 81920 | tf_op jit(solution)/shard_map/reduce_scatter | solution.py:45
  117.6 52.1 %reduce-scatter.21.cloned.1.call-start = ((), (), s32[]{:S(2)}) async-start(), calls=%async_computation.16 | async-start | bytes 163840 | tf_op jit(solution)/shard_map/reduce_scatter | solution.py:21
  150.1 52.3 %reduce-scatter.23.cloned.1.call-start = ((), (), s32[]{:S(2)}) async-start(), calls=%async_computation.17 | async-start | bytes 81920 | tf_op jit(solution)/shard_map/reduce_scatter | solution.py:45
  184.5 52.1 %reduce-scatter.25.cloned.1.call-start = ((), (), s32[]{:S(2)}) async-start(), calls=%async_computation.18 | async-start | bytes 163840 | tf_op jit(solution)/shard_map/reduce_scatter | solution.py:21
  217.0 52.3 %reduce-scatter.27.cloned.1.call-start = ((), (), s32[]{:S(2)}) async-start(), calls=%async_computation.19 | async-start | bytes 81920 | tf_op jit(solution)/shard_map/reduce_scatter | solution.py:45
  251.4 52.1 %reduce-scatter.29.cloned.1.call-start = ((), (), s32[]{:S(2)}) async-start(), calls=%async_computation.20 | async-start | bytes 163840 | tf_op jit(solution)/shard_map/reduce_scatter | solution.py:21
  283.9 52.3 %reduce-scatter.31.cloned.1.call-start = ((), (), s32[]{:S(2)}) async-start(), calls=%async_computation.21 | async-start | bytes 81920 | tf_op jit(solution)/shard_map/reduce_scatter | solution.py:45
  318.3 52.1 %reduce-scatter.33.cloned.1.call-start = ((), (), s32[]{:S(2)}) async-start(), calls=%async_computation.22 | async-start | bytes 163840 | tf_op jit(solution)/shard_map/reduce_scatter | solution.py:21
  350.7 52.3 %reduce-scatter.35.cloned.1.call-start = ((), (), s32[]{:S(2)}) async-start(), calls=%async_computation.23 | async-start | bytes 81920 | tf_op jit(solution)/shard_map/reduce_scatter | solution.py:45
  404.5 6.8 %copy-start.5 = (f32[32,128]{1,0:T(8,128)S(1)}, f32[32,128]{1,0:T(8,128)}, u32[]{:S(2)}) copy-start(f32[32,128]{1,0:T(8,128)} %reduce-scatter.35.cloned.1.call-done) | copy-start | bytes 49156
Sparse Core Ops, SparseCore 0:
  14.7 21.1 reduce-scatter.12
  50.9 17.7 reduce-scatter.14
  83.3 19.4 reduce-scatter.16
  117.7 17.7 reduce-scatter.18
  150.2 19.4 reduce-scatter.20
  184.6 17.7 reduce-scatter.22
  217.1 19.4 reduce-scatter.24
  251.5 17.7 reduce-scatter.26
  284.0 19.4 reduce-scatter.28
  318.4 17.7 reduce-scatter.30
  350.9 19.4 reduce-scatter.32
  385.3 17.7 reduce-scatter.34
where the time goes:
time: 420 us; the launch traced here: 419 us
  waiting for transfers between devices  223 us (53%)
  blocking collectives  144 us (34%)
  between operations  21.7 us (5%)
  other arithmetic  17.7 us (4%)
  matrix products  11.8 us (3%)
    reduce_scatter x6, waiting for transfers between devices, residual_of(): lax.psum_scatter(partial_value, 'pix', scatter_dimension=1, tiled=True)  119 us
    reduce_scatter x6, waiting for transfers between devices, on_device(): lax.psum_scatter(gradient_portion, 'base', scatter_dimension=1, tiled=True)  103 us
    all_gather x6, blocking collectives, residual_of(): lax.all_gather((own_rows - shares).astype(jnp.bfloat16), 'pix', axis=1, t...  78.7 us
    psum x6, blocking collectives, on_device(): total = lax.psum(local_sum, 'freq')  33.2 us
    all_gather x6, blocking collectives, on_device(): lax.all_gather(rounded_amount, 'base', axis=1, tiled=True)  32 us
    reduce_sum x6, other arithmetic, on_device(): local_sum = jnp.sum(tiles * tiles, axis=(0, 2))  8.45 us
  transfers between devices with their start and end apart: 12, of which 12 were waited for; matrix products, arithmetic and copies ran while one was open for 1% of the time, Pallas kernels for 0%

commit v1 on v0

--- a/solution.py
+++ b/solution.py
@@ -46,7 +46,7 @@
         moved = current + descent_stride * grad_share
         tiles = moved.reshape(chans, tiles_share, TILE)
         local_sum = jnp.sum(tiles * tiles, axis=(0, 2))
-        total = lax.psum(local_sum, "freq")
+        total = jnp.sum(lax.all_gather(local_sum, "freq"), axis=0)
         ranks = lax.dynamic_slice_in_dim(
             patch_order_record[step], base_index * tiles_share, tiles_share, 0
         )

time: 420 us -> 429 us (1.021)
  local copies, waits for them, and re-layouts: 0.69 us -> 10.5 us
    psum x6 -> x0, blocking collectives: 33.2 us -> none  [on_device(): total = lax.psum(local_sum, 'freq')]
    unnamed x0 -> x6, blocking collectives: none -> 29.5 us
    unnamed x12 -> x27, local copies, waits for them, and re-layouts: 0.62 us -> 10.5 us
where the time goes in v1:
time: 429 us; the launch traced here: 428 us
  waiting for transfers between devices  223 us (52%)
  blocking collectives  140 us (33%)
  between operations  21.9 us (5%)
  other arithmetic  20.1 us (5%)
  matrix products  11.8 us (3%)
  local copies, waits for them, and re-layouts  10.5 us (2%)
    reduce_scatter x6, waiting for transfers between devices, residual_of(): lax.psum_scatter(partial_value, 'pix', scatter_dimension=1, tiled=True)  118 us
    reduce_scatter x6, waiting for transfers between devices, on_device(): lax.psum_scatter(gradient_portion, 'base', scatter_dimension=1, tiled=True)  105 us
    all_gather x6, blocking collectives, residual_of(): lax.all_gather((own_rows - shares).astype(jnp.bfloat16), 'pix', axis=1, t...  78.7 us
    all_gather x6, blocking collectives, on_device(): lax.all_gather(rounded_amount, 'base', axis=1, tiled=True)  32 us
    unnamed x6, blocking collectives  29.5 us
    unnamed x27, local copies, waits for them, and re-layouts  10.5 us
  transfers between devices with their start and end apart: 12, of which 12 were waited for; matrix products, arithmetic and copies ran while one was open for 1% of the time, Pallas kernels for 0%

profile of v1, /device:TPU:0, one launch (start us, length us, event | category | flops | bytes accessed | tf_op | source)
XLA Modules:
  0.0 427.7 jit_solution(5896169883992012230)
XLA Ops:
  7.3 6.1 %all_gather.72 = bf16[32,512]{1,0:T(8,128)(2,1)S(1)} all-gather(bf16[32,128]{1,0:T(8,128)(2,1)S(1)} %convert_element_type.42), channel_id=1, replica_groups=mesh['freq'=2,'base'=4,'pix'=4] {'base'}, dimensions={1}, use_global_device_ids=true | all-gather | bytes 40960 | tf_op jit(solution)/shard_map/all_gather | solution.py:41
  15.9 20.0 %reduce-scatter.13.cloned.1.call-done = f32[32,256]{1,0:T(8,128)} async-done(((f32[32,1024]{1,0:T(8,128)}), f32[32,256]{1,0:T(8,128)}) %reduce-scatter.13.cloned.1.call-update) | async-done | bytes 32784 | tf_op jit(solution)/shard_map/reduce_scatter | solution.py:21
  36.7 13.1 %all_gather.73 = bf16[32,1024]{1,0:T(8,128)(2,1)S(1)} all-gather(bf16[32,256]{1,0:T(8,128)(2,1)S(1)} %subtract_convert_fusion.5), channel_id=1, replica_groups=mesh['freq'=2,'base'=4,'pix'=4] {'pix'}, dimensions={1}, use_global_device_ids=true | all-gather | bytes 81920 | tf_op jit(solution)/shard_map/all_gather | solution.py:26
  52.0 16.6 %reduce-scatter.15.cloned.1.call-done = f32[32,128]{1,0:T(8,128)} async-done(((f32[32,512]{1,0:T(8,128)}), f32[32,128]{1,0:T(8,128)}) %reduce-scatter.15.cloned.1.call-update) | async-done | bytes 16400 | tf_op jit(solution)/shard_map/reduce_scatter | solution.py:45
  70.1 1.4 dynamic-update-slice
  71.5 4.9 %all-reduce = f32[2]{0:T(128)S(1)} all-reduce(f32[2]{0:T(128)S(1)} %dynamic-update-slice), channel_id=1, replica_groups=mesh['freq'=2,'base'=4,'pix'=4] {'freq'}, use_global_device_ids=true, to_apply=%add | all-reduce | flops 2 | bytes 16
  78.5 5.2 %all_gather.76 = bf16[32,512]{1,0:T(8,128)(2,1)S(1)} all-gather(bf16[32,128]{1,0:T(8,128)(2,1)S(1)} %multiply_convert_fusion.4), channel_id=1, replica_groups=mesh['freq'=2,'base'=4,'pix'=4] {'base'}, dimensions={1}, use_global_device_ids=true | all-gather | bytes 40960 | tf_op jit(solution)/shard_map/all_gather | solution.py:41
  84.8 19.6 %reduce-scatter.17.cloned.1.call-done = f32[32,256]{1,0:T(8,128)} async-done(((f32[32,1024]{1,0:T(8,128)}), f32[32,256]{1,0:T(8,128)}) %reduce-scatter.17.cloned.1.call-update) | async-done | bytes 32784 | tf_op jit(solution)/shard_map/reduce_scatter | solution.py:21
  105.2 13.1 %all_gather.77 = bf16[32,1024]{1,0:T(8,128)(2,1)S(1)} all-gather(bf16[32,256]{1,0:T(8,128)(2,1)S(1)} %subtract_convert_fusion.4), channel_id=1, replica_groups=mesh['freq'=2,'base'=4,'pix'=4] {'pix'}, dimensions={1}, use_global_device_ids=true | all-gather | bytes 81920 | tf_op jit(solution)/shard_map/all_gather | solution.py:26
  119.8 17.3 %reduce-scatter.19.cloned.1.call-done = f32[32,128]{1,0:T(8,128)} async-done(((f32[32,512]{1,0:T(8,128)}), f32[32,128]{1,0:T(8,128)}) %reduce-scatter.19.cloned.1.call-update) | async-done | bytes 16400 | tf_op jit(solution)/shard_map/reduce_scatter | solution.py:45
  139.9 4.9 %all-reduce.1 = f32[2]{0:T(128)S(1)} all-reduce(f32[2]{0:T(128)S(1)} %dynamic-update-slice.1), channel_id=1, replica_groups=mesh['freq'=2,'base'=4,'pix'=4] {'freq'}, use_global_device_ids=true, to_apply=%add.1 | all-reduce | flops 2 | bytes 16
  146.7 5.2 %all_gather.80 = bf16[32,512]{1,0:T(8,128)(2,1)S(1)} all-gather(bf16[32,128]{1,0:T(8,128)(2,1)S(1)} %multiply_convert_fusion.3), channel_id=1, replica_groups=mesh['freq'=2,'base'=4,'pix'=4] {'base'}, dimensions={1}, use_global_device_ids=true | all-gather | bytes 40960 | tf_op jit(solution)/shard_map/all_gather | solution.py:41
  153.0 19.6 %reduce-scatter.21.cloned.1.call-done = f32[32,256]{1,0:T(8,128)} async-done(((f32[32,1024]{1,0:T(8,128)}), f32[32,256]{1,0:T(8,128)}) %reduce-scatter.21.cloned.1.call-update) | async-done | bytes 32784 | tf_op jit(solution)/shard_map/reduce_scatter | solution.py:21
  173.4 13.1 %all_gather.81 = bf16[32,1024]{1,0:T(8,128)(2,1)S(1)} all-gather(bf16[32,256]{1,0:T(8,128)(2,1)S(1)} %subtract_convert_fusion.3), channel_id=1, replica_groups=mesh['freq'=2,'base'=4,'pix'=4] {'pix'}, dimensions={1}, use_global_device_ids=true | all-gather | bytes 81920 | tf_op jit(solution)/shard_map/all_gather | solution.py:26
  187.5 17.8 %reduce-scatter.23.cloned.1.call-done = f32[32,128]{1,0:T(8,128)} async-done(((f32[32,512]{1,0:T(8,128)}), f32[32,128]{1,0:T(8,128)}) %reduce-scatter.23.cloned.1.call-update) | async-done | bytes 16400 | tf_op jit(solution)/shard_map/reduce_scatter | solution.py:45
  208.1 4.9 %all-reduce.2 = f32[2]{0:T(128)S(1)} all-reduce(f32[2]{0:T(128)S(1)} %dynamic-update-slice.2), channel_id=1, replica_groups=mesh['freq'=2,'base'=4,'pix'=4] {'freq'}, use_global_device_ids=true, to_apply=%add.2 | all-reduce | flops 2 | bytes 16
  215.2 5.2 %all_gather.84 = bf16[32,512]{1,0:T(8,128)(2,1)S(1)} all-gather(bf16[32,128]{1,0:T(8,128)(2,1)S(1)} %multiply_convert_fusion.2), channel_id=1, replica_groups=mesh['freq'=2,'base'=4,'pix'=4] {'base'}, dimensions={1}, use_global_device_ids=true | all-gather | bytes 40960 | tf_op jit(solution)/shard_map/all_gather | solution.py:41
  221.5 19.6 %reduce-scatter.25.cloned.1.call-done = f32[32,256]{1,0:T(8,128)} async-done(((f32[32,1024]{1,0:T(8,128)}), f32[32,256]{1,0:T(8,128)}) %reduce-scatter.25.cloned.1.call-update) | async-done | bytes 32784 | tf_op jit(solution)/shard_map/reduce_scatter | solution.py:21
  241.8 13.1 %all_gather.85 = bf16[32,1024]{1,0:T(8,128)(2,1)S(1)} all-gather(bf16[32,256]{1,0:T(8,128)(2,1)S(1)} %subtract_convert_fusion.2), channel_id=1, replica_groups=mesh['freq'=2,'base'=4,'pix'=4] {'pix'}, dimensions={1}, use_global_device_ids=true | all-gather | bytes 81920 | tf_op jit(solution)/shard_map/all_gather | solution.py:26
  256.4 17.3 %reduce-scatter.27.cloned.1.call-done = f32[32,128]{1,0:T(8,128)} async-done(((f32[32,512]{1,0:T(8,128)}), f32[32,128]{1,0:T(8,128)}) %reduce-scatter.27.cloned.1.call-update) | async-done | bytes 16400 | tf_op jit(solution)/shard_map/reduce_scatter | solution.py:45
  276.6 4.9 %all-reduce.3 = f32[2]{0:T(128)S(1)} all-reduce(f32[2]{0:T(128)S(1)} %dynamic-update-slice.3), channel_id=1, replica_groups=mesh['freq'=2,'base'=4,'pix'=4] {'freq'}, use_global_device_ids=true, to_apply=%add.3 | all-reduce | flops 2 | bytes 16
  283.3 5.2 %all_gather.88 = bf16[32,512]{1,0:T(8,128)(2,1)S(1)} all-gather(bf16[32,128]{1,0:T(8,128)(2,1)S(1)} %multiply_convert_fusion.1), channel_id=1, replica_groups=mesh['freq'=2,'base'=4,'pix'=4] {'base'}, dimensions={1}, use_global_device_ids=true | all-gather | bytes 40960 | tf_op jit(solution)/shard_map/all_gather | solution.py:41
  289.7 19.6 %reduce-scatter.29.cloned.1.call-done = f32[32,256]{1,0:T(8,128)} async-done(((f32[32,1024]{1,0:T(8,128)}), f32[32,256]{1,0:T(8,128)}) %reduce-scatter.29.cloned.1.call-update) | async-done | bytes 32784 | tf_op jit(solution)/shard_map/reduce_scatter | solution.py:21
  310.0 13.1 %all_gather.89 = bf16[32,1024]{1,0:T(8,128)(2,1)S(1)} all-gather(bf16[32,256]{1,0:T(8,128)(2,1)S(1)} %subtract_convert_fusion.1), channel_id=1, replica_groups=mesh['freq'=2,'base'=4,'pix'=4] {'pix'}, dimensions={1}, use_global_device_ids=true | all-gather | bytes 81920 | tf_op jit(solution)/shard_map/all_gather | solution.py:26
  324.1 17.8 %reduce-scatter.31.cloned.1.call-done = f32[32,128]{1,0:T(8,128)} async-done(((f32[32,512]{1,0:T(8,128)}), f32[32,128]{1,0:T(8,128)}) %reduce-scatter.31.cloned.1.call-update) | async-done | bytes 16400 | tf_op jit(solution)/shard_map/reduce_scatter | solution.py:45
  344.7 4.9 %all-reduce.4 = f32[2]{0:T(128)S(1)} all-reduce(f32[2]{0:T(128)S(1)} %dynamic-update-slice.4), channel_id=1, replica_groups=mesh['freq'=2,'base'=4,'pix'=4] {'freq'}, use_global_device_ids=true, to_apply=%add.4 | all-reduce | flops 2 | bytes 16
  351.8 5.2 %all_gather.92 = bf16[32,512]{1,0:T(8,128)(2,1)S(1)} all-gather(bf16[32,128]{1,0:T(8,128)(2,1)S(1)} %multiply_convert_fusion), channel_id=1, replica_groups=mesh['freq'=2,'base'=4,'pix'=4] {'base'}, dimensions={1}, use_global_device_ids=true | all-gather | bytes 40960 | tf_op jit(solution)/shard_map/all_gather | solution.py:41
  358.1 19.5 %reduce-scatter.33.cloned.1.call-done = f32[32,256]{1,0:T(8,128)} async-done(((f32[32,1024]{1,0:T(8,128)}), f32[32,256]{1,0:T(8,128)}) %reduce-scatter.33.cloned.1.call-update) | async-done | bytes 32784 | tf_op jit(solution)/shard_map/reduce_scatter | solution.py:21
  378.4 13.1 %all_gather.93 = bf16[32,1024]{1,0:T(8,128)(2,1)S(1)} all-gather(bf16[32,256]{1,0:T(8,128)(2,1)S(1)} %subtract_convert_fusion), channel_id=1, replica_groups=mesh['freq'=2,'base'=4,'pix'=4] {'pix'}, dimensions={1}, use_global_device_ids=true | all-gather | bytes 81920 | tf_op jit(solution)/shard_map/all_gather | solution.py:26
  392.4 17.9 %reduce-scatter.35.cloned.1.call-done = f32[32,128]{1,0:T(8,128)} async-done(((f32[32,512]{1,0:T(8,128)}), f32[32,128]{1,0:T(8,128)}) %reduce-scatter.35.cloned.1.call-update) | async-done | bytes 16400 | tf_op jit(solution)/shard_map/reduce_scatter | solution.py:45
  411.8 1.4 dynamic-update-slice.5
  413.2 4.9 %all-reduce.5 = f32[2]{0:T(128)S(1)} all-reduce(f32[2]{0:T(128)S(1)} %dynamic-update-slice.5), channel_id=1, replica_groups=mesh['freq'=2,'base'=4,'pix'=4] {'freq'}, use_global_device_ids=true, to_apply=%add.5 | all-reduce | flops 2 | bytes 16
  (90 shorter events, 40.1 us)
Async XLA Ops:
  6.5 7.0 %copy-start = (bf16[1,1024,512]{2,1,0:T(8,128)(2,1)S(1)}, bf16[1,1024,512]{2,1,0:T(8,128)(2,1)}, u32[]{:S(2)}) copy-start(bf16[1,1024,512]{2,1,0:T(8,128)(2,1)} %param.4) | copy-start | bytes 3145732
  6.5 29.4 %reduce-scatter.13.cloned.1.call-start = ((), (), s32[]{:S(2)}) async-start(), calls=%async_computation.12 | async-start | bytes 163840 | tf_op jit(solution)/shard_map/reduce_scatter | solution.py:21
  14.5 21.4 %copy-start.1 = (f32[32,1024]{1,0:T(8,128)S(1)}, f32[32,1024]{1,0:T(8,128)}, u32[]{:S(2)}) copy-start(f32[32,1024]{1,0:T(8,128)} %param.5) | copy-start | bytes 393220
  14.6 54.1 %reduce-scatter.15.cloned.1.call-start = ((), (), s32[]{:S(2)}) async-start(), calls=%async_computation.13 | async-start | bytes 81920 | tf_op jit(solution)/shard_map/reduce_scatter | solution.py:45
  14.6 0.7 copy-start.6
  50.7 0.7 copy-start.4
  50.8 17.9 %copy-start.2 = (f32[32,1,1,128]{3,2,1,0:T(1,128)S(1)}, f32[32,1,1,128]{3,2,1,0:T(1,128)}, u32[]{:S(2)}) copy-start(f32[32,1,1,128]{3,2,1,0:T(1,128)} %param.6) | copy-start | bytes 49156
  50.8 53.6 %reduce-scatter.17.cloned.1.call-start = ((), (), s32[]{:S(2)}) async-start(), calls=%async_computation.14 | async-start | bytes 163840 | tf_op jit(solution)/shard_map/reduce_scatter | solution.py:21
  70.1 8.4 %copy-start.3 = (f32[32,128]{1,0:T(8,128)S(1)}, f32[32,128]{1,0:T(8,128)}, u32[]{:S(2)}) copy-start(f32[32,128]{1,0:T(8,128)} %reduce-scatter.15.cloned.1.call-done) | copy-start | bytes 49156
  84.8 52.3 %reduce-scatter.19.cloned.1.call-start = ((), (), s32[]{:S(2)}) async-start(), calls=%async_computation.15 | async-start | bytes 81920 | tf_op jit(solution)/shard_map/reduce_scatter | solution.py:45
  119.2 53.4 %reduce-scatter.21.cloned.1.call-start = ((), (), s32[]{:S(2)}) async-start(), calls=%async_computation.16 | async-start | bytes 163840 | tf_op jit(solution)/shard_map/reduce_scatter | solution.py:21
  153.0 52.3 %reduce-scatter.23.cloned.1.call-start = ((), (), s32[]{:S(2)}) async-start(), calls=%async_computation.17 | async-start | bytes 81920 | tf_op jit(solution)/shard_map/reduce_scatter | solution.py:45
  187.4 53.6 %reduce-scatter.25.cloned.1.call-start = ((), (), s32[]{:S(2)}) async-start(), calls=%async_computation.18 | async-start | bytes 163840 | tf_op jit(solution)/shard_map/reduce_scatter | solution.py:21
  221.4 52.3 %reduce-scatter.27.cloned.1.call-start = ((), (), s32[]{:S(2)}) async-start(), calls=%async_computation.19 | async-start | bytes 81920 | tf_op jit(solution)/shard_map/reduce_scatter | solution.py:45
  255.8 53.4 %reduce-scatter.29.cloned.1.call-start = ((), (), s32[]{:S(2)}) async-start(), calls=%async_computation.20 | async-start | bytes 163840 | tf_op jit(solution)/shard_map/reduce_scatter | solution.py:21
  289.6 52.3 %reduce-scatter.31.cloned.1.call-start = ((), (), s32[]{:S(2)}) async-start(), calls=%async_computation.21 | async-start | bytes 81920 | tf_op jit(solution)/shard_map/reduce_scatter | solution.py:45
  324.0 53.6 %reduce-scatter.33.cloned.1.call-start = ((), (), s32[]{:S(2)}) async-start(), calls=%async_computation.22 | async-start | bytes 163840 | tf_op jit(solution)/shard_map/reduce_scatter | solution.py:21
  358.0 52.3 %reduce-scatter.35.cloned.1.call-start = ((), (), s32[]{:S(2)}) async-start(), calls=%async_computation.23 | async-start | bytes 81920 | tf_op jit(solution)/shard_map/reduce_scatter | solution.py:45
  411.8 8.5 %copy-start.5 = (f32[32,128]{1,0:T(8,128)S(1)}, f32[32,128]{1,0:T(8,128)}, u32[]{:S(2)}) copy-start(f32[32,128]{1,0:T(8,128)} %reduce-scatter.35.cloned.1.call-done) | copy-start | bytes 49156
Sparse Core Ops, SparseCore 0:
  14.7 21.1 reduce-scatter.12
  50.9 17.7 reduce-scatter.14
  84.9 19.4 reduce-scatter.16
  119.3 17.7 reduce-scatter.18
  153.1 19.4 reduce-scatter.20
  187.5 17.7 reduce-scatter.22
  221.5 19.4 reduce-scatter.24
  256.0 17.7 reduce-scatter.26
  289.7 19.4 reduce-scatter.28
  324.1 17.7 reduce-scatter.30
  358.1 19.4 reduce-scatter.32
  392.5 17.7 reduce-scatter.34
